TPU v7x, 32 devices: a whole 2x2x4 slice. The times are simulated.
32 devices in a mesh: gx: 4 (over y, core), gy: 2 (over x), gz: 4 (over z).
Axes of the slice: x: 2, y: 2, z: 4, core: 2. Of those that a mesh axis runs over, the one named last changes fastest.
Arguments:
- positions: float32 [3, 4096, 128], P(None, ('gx', 'gy', 'gz')), may hold values from 0 to 1, as said below
- charges: float32 [4096, 128], P(('gx', 'gy', 'gz')), may hold values from -6 to 6
- velocities: float32 [3, 4096, 128], P(None, ('gx', 'gy', 'gz')), may hold values from -6 to 6
- leaf_ids: int32 [4096], P(('gx', 'gy', 'gz')), may hold values from 0 to 2097151, as said below
- live_counts: int32 [32], replicated, may hold values from 32 to 96
- send_counts: int32 [5, 32], replicated, may hold values from 0 to 32, as said below
Outputs:
- moved_positions: float32 [3, 4096, 128], P(None, ('gx', 'gy', 'gz'))
- moved_charges: float32 [4096, 128], P(('gx', 'gy', 'gz'))
- moved_velocities: float32 [3, 4096, 128], P(None, ('gx', 'gy', 'gz'))
- moved_leaves: int32 [4096], P(('gx', 'gy', 'gz'))
- leaf_moments: float32 [286, 4096], P(None, ('gx', 'gy', 'gz'))
- parent_moments: float32 [286, 4096], P(None, ('gx', 'gy', 'gz'))
Inputs may be any that keep to these rules, and one draw needn't show every extreme that they name: `positions`: every particle of a live slot lies inside the leaf cell of side 2^-7 named by the slot's leaf index. `leaf_ids`: morton indices of cells at depth 7; a leaf's parent cell is its index // 8. `send_counts`: no device sends more blocks than it holds live; after every section no device holds more than 128 live blocks; in every draw some device sends exactly 32 blocks in the first section and its partner then holds exactly 128.
All inputs are finite; a program needn't handle non-finite values.
Results may differ from a plain program's by a relative error of at most 0.0003.
Values sent between devices are 32-bit elements; how exact they have to be, the bound alone decides.
A program may use at most 128 MiB of HBM per device.

v0:
```python
import functools
import math

import jax
import jax.numpy as jnp
import numpy as np
from jax import lax
from jax.experimental import pallas as pl
from jax.experimental.pallas import tpu as pltpu
from jax.sharding import PartitionSpec as P

ORDER = 10
LEVEL = 7
AXES = ("gx", "gy", "gz")
TILE = 8


def exponents(max_order):
    return [
        (p, q, r)
        for p in range(max_order + 1)
        for q in range(max_order + 1 - p)
        for r in range(max_order + 1 - p - q)
    ]


def shift_constants(max_order, rows, lanes):
    triples = exponents(max_order)
    table = np.zeros((rows, rows))
    parity = np.zeros((rows, lanes), np.int32)
    for k, (p, q, r) in enumerate(triples):
        parity[k] = (p & 1) * 4 + (q & 1) * 2 + (r & 1)
        for j, (e, f, g) in enumerate(triples):
            if e <= p and f <= q and g <= r:
                ways = math.comb(p, e) * math.comb(q, f) * math.comb(r, g)
                table[k, j] = ways * 0.5 ** (p + q + r)
    return jnp.asarray(table, jnp.bfloat16), jnp.asarray(parity)


def exchange_kernel(
    sizes,
    live_ref,
    sends_ref,
    leaf_ref,
    pos_ref,
    chg_ref,
    vel_ref,
    out_ref,
    leaf_out_ref,
    state_a,
    state_b,
    send_a,
    send_b,
    in_sem,
    send_sem,
    recv_sem,
    *recv_all,
):
    nx, ny, nz = sizes
    recv_a, recv_b = recv_all[0::2], recv_all[1::2]
    sections = (nx * ny * nz).bit_length() - 1
    slots, part = chg_ref.shape
    slab = slots // 4
    pad = slab
    groups = ((state_a, send_a, recv_a, 4, 0), (state_b, send_b, recv_b, 3, 4))
    device = (lax.axis_index("gx") * ny + lax.axis_index("gy")) * nz + lax.axis_index("gz")

    loads = [
        pltpu.make_async_copy(pos_ref, state_a.at[0, 0:3, pad : pad + slots, :], in_sem.at[0]),
        pltpu.make_async_copy(chg_ref, state_a.at[0, 3, pad : pad + slots, :], in_sem.at[1]),
        pltpu.make_async_copy(vel_ref, state_b.at[0, 0:3, pad : pad + slots, :], in_sem.at[2]),
    ]
    for load in loads:
        load.start()

    masks = [1 << (sections - 1 - s) for s in range(sections)]
    uppers = [lax.rem(lax.div(device, m), 2) for m in masks]
    partners = [device + m - 2 * m * up for m, up in zip(masks, uppers)]
    places = [
        (lax.div(e, ny * nz), lax.rem(lax.div(e, nz), ny), lax.rem(e, nz)) for e in partners
    ]

    barrier = pltpu.get_barrier_semaphore()
    for place in places:
        pl.semaphore_signal(
            barrier, inc=1, device_id=place, device_id_type=pl.DeviceIdType.MESH
        )

    live = live_ref[device]
    plans = []
    for s in range(sections):
        sent = sends_ref[s, device]
        got = sends_ref[s, partners[s]]
        up = uppers[s]
        kept = live - sent
        start = (1 - up) * kept
        old_by = up * (sent - got)
        new_at = (1 - up) * kept
        plans.append((start, old_by, new_at, got))
        live = kept + got

    for state, send, recv, members, _ in groups:
        edge = jnp.zeros((members, pad, part), jnp.float32)
        for side in range(2):
            state[side, :, 0:pad, :] = edge
            state[side, :, pad + slots : 2 * pad + slots, :] = edge
        rows = TILE + members * slab
        for s in range(sections):
            recv[s][rows : rows + TILE, :] = jnp.zeros((TILE, part), jnp.float32)
    for s in range(sections):
        send_b[s, 0:TILE, :] = jnp.zeros((TILE, part), jnp.float32)

    leaf = jnp.broadcast_to(leaf_ref[...], (TILE, slots)).astype(jnp.float32)
    lane = lax.broadcasted_iota(jnp.int32, (TILE, slots), 1)
    row = lax.broadcasted_iota(jnp.int32, (TILE, part), 0)

    def copy_of(s, g):
        _, send, recv, members, _ = groups[g]
        rows = TILE + members * slab
        return pltpu.make_async_remote_copy(
            src_ref=send.at[s],
            dst_ref=recv[s].at[0:rows, :],
            send_sem=send_sem.at[s, g],
            recv_sem=recv_sem.at[s, g],
            device_id=places[s],
            device_id_type=pl.DeviceIdType.MESH,
        )

    def emit(s, g, leaf):
        state, send, _, members, _ = groups[g]
        start = plans[s][0]
        if g == 0:
            send[s, 0:TILE, :] = pltpu.roll(leaf, lax.rem(slots - start, slots), 1)
        for m in range(members):
            at = TILE + m * slab
            send[s, at : at + slab, :] = state[s % 2, m, pl.ds(pad + start, slab), :]
        copy = copy_of(s, g)
        copy.start()
        return copy

    def merge(s, g):
        state, _, recv, members, first = groups[g]
        _, old_by, new_at, got = plans[s]
        last = s == sections - 1
        for t in range(slots // TILE):
            base = TILE * t - new_at
            window = jnp.clip(base, -TILE, slab) + TILE
            index = row + base
            fresh = (index >= 0) & (index < got)
            filled = row + TILE * t < live
            for m in range(members):
                old = state[s % 2, m, pl.ds(pad + TILE * t + old_by, TILE), :]
                new = recv[s][pl.ds(window + m * slab, TILE), :]
                value = jnp.where(fresh, new, old)
                if last:
                    value = jnp.where(filled, value, 0.0)
                    out_ref[first + m, TILE * t : TILE * t + TILE, :] = value
                else:
                    at = pad + TILE * t
                    state[1 - s % 2, m, at : at + TILE, :] = value

    def merge_leaf(s, leaf):
        _, old_by, new_at, got = plans[s]
        old = pltpu.roll(leaf, lax.rem(slots - old_by, slots), 1)
        new = pltpu.roll(recv_a[s][0:TILE, :], lax.rem(new_at, slots), 1)
        index = lane - new_at
        return jnp.where((index >= 0) & (index < got), new, old)

    loads[0].wait()
    loads[1].wait()
    loads[2].wait()
    pl.semaphore_wait(barrier, sections)

    first = emit(0, 0, leaf)
    second = emit(0, 1, leaf)
    started = []
    for s in range(sections):
        first.wait_recv()
        started += [first, second]
        leaf = merge_leaf(s, leaf)
        merge(s, 0)
        if s + 1 < sections:
            first = emit(s + 1, 0, leaf)
        second.wait_recv()
        merge(s, 1)
        if s + 1 < sections:
            second = emit(s + 1, 1, leaf)
    leaf_out_ref[...] = jnp.where(lane < live, leaf, -1.0)
    for copy in started:
        copy.wait_send()


def moments_kernel(
    max_order,
    depth,
    moved_ref,
    leaf_ref,
    table_ref,
    parity_ref,
    pos_ref,
    chg_ref,
    vel_ref,
    leaves_ref,
    moments_ref,
    parents_ref,
    trans,
    acc,
):
    slots, part = chg_ref.shape
    count = moments_ref.shape[0]
    rows = table_ref.shape[0]
    pos_ref[...] = moved_ref[0:3]
    chg_ref[...] = moved_ref[3]
    vel_ref[...] = moved_ref[4:7]
    found = leaf_ref[0:1, :].astype(jnp.int32)
    leaves_ref[...] = found
    alive = found >= 0
    leaves = jnp.where(alive, found, 0)

    for axis in range(3):
        cell = jnp.zeros_like(leaves)
        for level in range(depth):
            bit = jnp.bitwise_and(jnp.right_shift(leaves, 3 * level + 2 - axis), 1)
            cell = cell + jnp.left_shift(bit, level)
        spots = moved_ref[axis].T
        trans[axis] = 2.0 * (spots * float(2**depth) - cell.astype(jnp.float32)) - 1.0
    trans[3] = moved_ref[3].T

    acc[...] = jnp.zeros_like(acc)
    chunk = 64

    def body(h, carry):
        at = pl.ds(pl.multiple_of(h * chunk, chunk), chunk)
        u = trans[0, at, :]
        v = trans[1, at, :]
        w = trans[2, at, :]
        a = trans[3, at, :]
        k = 0
        for p in range(max_order + 1):
            b = a
            for q in range(max_order + 1 - p):
                d = b
                for r in range(max_order + 1 - p - q):
                    total = d[0:TILE]
                    for n in range(1, chunk // TILE):
                        total = total + d[n * TILE : n * TILE + TILE]
                    acc[k * TILE : k * TILE + TILE, :] += total
                    k += 1
                    if r < max_order - p - q:
                        d = d * w
                if q < max_order - p:
                    b = b * v
            if p < max_order:
                a = a * u
        return carry

    lax.fori_loop(0, part // chunk, body, 0)

    sums = acc[pl.ds(0, rows, stride=TILE), :]
    for n in range(1, TILE):
        sums = sums + acc[pl.ds(n, rows, stride=TILE), :]
    moments = sums * (1.0 / 16.0)
    moments_ref[...] = moments[:count]

    minus = 7 - jnp.bitwise_and(leaves, 7)
    odd = jnp.bitwise_and(parity_ref[...], minus)
    odd = jnp.bitwise_xor(jnp.bitwise_xor(odd, jnp.right_shift(odd, 1)), jnp.right_shift(odd, 2))
    flip = jnp.bitwise_and(odd, 1) == 1

    def dot(table, value, swap):
        parts = []
        rest = value
        for _ in range(3):
            piece = rest.astype(jnp.bfloat16)
            rest = rest - piece.astype(jnp.float32)
            parts.append(piece)
        result = 0.0
        for piece in parts[::-1]:
            left, right = (piece, table) if swap else (table, piece)
            result = result + jnp.dot(left, right, preferred_element_type=jnp.float32)
        return result

    lifted = dot(table_ref[...], jnp.where(flip, -moments, moments), False)
    lifted = jnp.where(flip, -lifted, lifted)
    parent = jnp.right_shift(leaves, 3).astype(jnp.float32)
    across = jnp.broadcast_to(jnp.where(alive, parent, -1.0), (slots, slots))
    down = jnp.broadcast_to(jnp.where(alive, parent, -2.0), (slots, slots)).T
    sibling = (across == down).astype(jnp.bfloat16)
    parents_ref[...] = dot(sibling, lifted, True)[:count]


def per_device(sizes, positions, charges, velocities, leaf_ids, live_counts, send_counts):
    slots, part = charges.shape
    slab = slots // 4
    sections = (sizes[0] * sizes[1] * sizes[2]).bit_length() - 1
    f32 = jnp.float32
    any_space = pl.BlockSpec(memory_space=pl.ANY)
    vmem = pl.BlockSpec(memory_space=pltpu.VMEM)
    smem = pl.BlockSpec(memory_space=pltpu.SMEM)
    rows_a = TILE + 4 * slab
    rows_b = TILE + 3 * slab
    moved, leaf = pl.pallas_call(
        functools.partial(exchange_kernel, sizes),
        out_shape=(
            jax.ShapeDtypeStruct((7, slots, part), f32),
            jax.ShapeDtypeStruct((TILE, slots), f32),
        ),
        in_specs=[smem, smem, vmem, any_space, any_space, any_space],
        out_specs=(vmem, vmem),
        scratch_shapes=[
            pltpu.VMEM((2, 4, slots + 2 * slab, part), f32),
            pltpu.VMEM((2, 3, slots + 2 * slab, part), f32),
            pltpu.VMEM((sections, rows_a, part), f32),
            pltpu.VMEM((sections, rows_b, part), f32),
            pltpu.SemaphoreType.DMA((3,)),
            pltpu.SemaphoreType.DMA((sections, 2)),
            pltpu.SemaphoreType.DMA((sections, 2)),
        ]
        + [pltpu.VMEM((r + TILE, part), f32) for _ in range(sections) for r in (rows_a, rows_b)],
        compiler_params=pltpu.CompilerParams(collective_id=0, has_side_effects=True),
    )(live_counts, send_counts, leaf_ids.reshape(1, slots), positions, charges, velocities)

    count = len(exponents(ORDER))
    rows = -(-count // 16) * 16
    table, parity = shift_constants(ORDER, rows, slots)
    outs = pl.pallas_call(
        functools.partial(moments_kernel, ORDER, LEVEL),
        out_shape=(
            jax.ShapeDtypeStruct(positions.shape, f32),
            jax.ShapeDtypeStruct(charges.shape, f32),
            jax.ShapeDtypeStruct(velocities.shape, f32),
            jax.ShapeDtypeStruct((1, slots), jnp.int32),
            jax.ShapeDtypeStruct((count, slots), f32),
            jax.ShapeDtypeStruct((count, slots), f32),
        ),
        in_specs=[vmem] * 4,
        out_specs=(vmem,) * 6,
        scratch_shapes=[
            pltpu.VMEM((4, part, slots), f32),
            pltpu.VMEM((rows * TILE, slots), f32),
        ],
    )(moved, leaf, table, parity)
    return (outs[0], outs[1], outs[2], outs[3].reshape(slots), outs[4], outs[5])


def solution(mesh):
    sizes = tuple(mesh.shape[name] for name in AXES)
    in_specs = (
        P(None, AXES, None),
        P(AXES, None),
        P(None, AXES, None),
        P(AXES),
        P(),
        P(),
    )
    out_specs = (
        P(None, AXES, None),
        P(AXES, None),
        P(None, AXES, None),
        P(AXES),
        P(None, AXES),
        P(None, AXES),
    )
    return jax.shard_map(
        functools.partial(per_device, sizes),
        mesh=mesh,
        in_specs=in_specs,
        out_specs=out_specs,
        check_vma=False,
    )
```

profile of v0, /device:TPU:0, one launch (start us, length us, event | category | flops | bytes accessed | tf_op | source)
XLA Modules:
  0.0 30.8 jit_solution(628865683430564672)
XLA Ops:
  0.6 26.2 %shard_map.127 = (f32[7,128,128]{2,1,0:T(8,128)}, f32[8,128]{1,0:T(8,128)}) custom-call(s32[32]{0:T(128)} %live_ref.1, s32[5,32]{1,0:T(8,128)} %sends_ref.1, s32[1,128]{1,0:T(1,128)} %bitcast.2, f32[3,128,128]{2,1,0:T(8,128)} %pos_ref.1, f32[128,128]{1,0:T(8,128)} %chg_ref.1, f32[3,128,128]{2,1,0:T(8,128)} %vel_ref.1), custom_call_target="tpu_custom_call" | custom-call | tf_op jit(solution)/shard_map/pallas_call | solution.py:302
  26.8 4.0 %shard_map.128 = (f32[3,128,128]{2,1,0:T(8,128)}, f32[128,128]{1,0:T(8,128)}, f32[3,128,128]{2,1,0:T(8,128)}, s32[1,128]{1,0:T(1,128)}, f32[286,128]{1,0:T(8,128)}, /*index=5*/f32[286,128]{1,0:T(8,128)}) custom-call(f32[7,128,128]{2,1,0:T(8,128)} %get-tuple-element.14.moved_ref, f32[8,128]{1,0:T(8,128)} %get-tuple-element.15.leaf_ref, ...), custom_call_target="tpu_custom_call" | custom-call | tf_op jit(solution)/shard_map/pallas_call | solution.py:326
where the time goes:
time: 31 us; the launch traced here: 30.8 us
  Pallas kernels  30.2 us (97%)
  between operations  0.64 us (2%)
    pallas_call x1, Pallas kernels, per_device(): pl.pallas_call(functools.partial(exchange_kernel, sizes), out_shape=(jax....  26.2 us
    pallas_call x1, Pallas kernels, per_device(): pl.pallas_call(functools.partial(moments_kernel, ORDER, LEVEL), out_shape...  4.01 us

commit v1 on v0

--- a/solution.py
+++ b/solution.py
@@ -13,6 +13,10 @@
 LEVEL = 7
 AXES = ("gx", "gy", "gz")
 TILE = 8
+MEMBERS = 7
+LEAF_CHAIN = 3
+CHAIN_ORDER = (3, 0, 1, 2, 4, 5, 6)
+SKEW = 3
 
 
 def exponents(max_order):
@@ -47,31 +51,27 @@
     vel_ref,
     out_ref,
     leaf_out_ref,
-    state_a,
-    state_b,
-    send_a,
-    send_b,
+    slabs,
     in_sem,
     send_sem,
     recv_sem,
-    *recv_all,
+    *buffers,
 ):
     nx, ny, nz = sizes
-    recv_a, recv_b = recv_all[0::2], recv_all[1::2]
     sections = (nx * ny * nz).bit_length() - 1
     slots, part = chg_ref.shape
     slab = slots // 4
     pad = slab
-    groups = ((state_a, send_a, recv_a, 4, 0), (state_b, send_b, recv_b, 3, 4))
+    states, arrivals = buffers[:MEMBERS], buffers[MEMBERS:]
     device = (lax.axis_index("gx") * ny + lax.axis_index("gy")) * nz + lax.axis_index("gz")
 
-    loads = [
-        pltpu.make_async_copy(pos_ref, state_a.at[0, 0:3, pad : pad + slots, :], in_sem.at[0]),
-        pltpu.make_async_copy(chg_ref, state_a.at[0, 3, pad : pad + slots, :], in_sem.at[1]),
-        pltpu.make_async_copy(vel_ref, state_b.at[0, 0:3, pad : pad + slots, :], in_sem.at[2]),
-    ]
-    for load in loads:
-        load.start()
+    sources = [pos_ref.at[0], pos_ref.at[1], pos_ref.at[2], chg_ref]
+    sources += [vel_ref.at[0], vel_ref.at[1], vel_ref.at[2]]
+    loads = []
+    for m in CHAIN_ORDER:
+        landing = states[m].at[0, pad : pad + slots, :]
+        loads.append(pltpu.make_async_copy(sources[m], landing, in_sem.at[m]))
+        loads[-1].start()
 
     masks = [1 << (sections - 1 - s) for s in range(sections)]
     uppers = [lax.rem(lax.div(device, m), 2) for m in masks]
@@ -95,98 +95,82 @@
         kept = live - sent
         start = (1 - up) * kept
         old_by = up * (sent - got)
-        new_at = (1 - up) * kept
-        plans.append((start, old_by, new_at, got))
+        plans.append((start, old_by, start, got))
         live = kept + got
 
-    for state, send, recv, members, _ in groups:
-        edge = jnp.zeros((members, pad, part), jnp.float32)
+    edge = jnp.zeros((pad, part), jnp.float32)
+    for m in range(MEMBERS):
         for side in range(2):
-            state[side, :, 0:pad, :] = edge
-            state[side, :, pad + slots : 2 * pad + slots, :] = edge
-        rows = TILE + members * slab
-        for s in range(sections):
-            recv[s][rows : rows + TILE, :] = jnp.zeros((TILE, part), jnp.float32)
+            states[m][side, 0:pad, :] = edge
+            states[m][side, pad + slots : 2 * pad + slots, :] = edge
     for s in range(sections):
-        send_b[s, 0:TILE, :] = jnp.zeros((TILE, part), jnp.float32)
-
-    leaf = jnp.broadcast_to(leaf_ref[...], (TILE, slots)).astype(jnp.float32)
+        for m in range(MEMBERS):
+            arrived = arrivals[s * MEMBERS + m]
+            if m != LEAF_CHAIN:
+                arrived[0:TILE, :] = edge[0:TILE]
+            arrived[TILE + slab : 2 * TILE + slab, :] = edge[0:TILE]
+
     lane = lax.broadcasted_iota(jnp.int32, (TILE, slots), 1)
     row = lax.broadcasted_iota(jnp.int32, (TILE, part), 0)
 
-    def copy_of(s, g):
-        _, send, recv, members, _ = groups[g]
-        rows = TILE + members * slab
-        return pltpu.make_async_remote_copy(
-            src_ref=send.at[s],
-            dst_ref=recv[s].at[0:rows, :],
-            send_sem=send_sem.at[s, g],
-            recv_sem=recv_sem.at[s, g],
+    def emit(s, m, leaf):
+        start = plans[s][0]
+        first = TILE
+        if m == LEAF_CHAIN:
+            slabs[s, m, 0:TILE, :] = pltpu.roll(leaf, lax.rem(slots - start, slots), 1)
+            first = 0
+        slabs[s, m, TILE : TILE + slab, :] = states[m][s % 2, pl.ds(pad + start, slab), :]
+        copy = pltpu.make_async_remote_copy(
+            src_ref=slabs.at[s, m, first : TILE + slab, :],
+            dst_ref=arrivals[s * MEMBERS + m].at[first : TILE + slab, :],
+            send_sem=send_sem.at[s, m],
+            recv_sem=recv_sem.at[s, m],
             device_id=places[s],
             device_id_type=pl.DeviceIdType.MESH,
         )
-
-    def emit(s, g, leaf):
-        state, send, _, members, _ = groups[g]
-        start = plans[s][0]
-        if g == 0:
-            send[s, 0:TILE, :] = pltpu.roll(leaf, lax.rem(slots - start, slots), 1)
-        for m in range(members):
-            at = TILE + m * slab
-            send[s, at : at + slab, :] = state[s % 2, m, pl.ds(pad + start, slab), :]
-        copy = copy_of(s, g)
         copy.start()
         return copy
 
-    def merge(s, g):
-        state, _, recv, members, first = groups[g]
+    def merge(s, m):
+        state, arrived = states[m], arrivals[s * MEMBERS + m]
         _, old_by, new_at, got = plans[s]
-        last = s == sections - 1
         for t in range(slots // TILE):
             base = TILE * t - new_at
             window = jnp.clip(base, -TILE, slab) + TILE
             index = row + base
             fresh = (index >= 0) & (index < got)
-            filled = row + TILE * t < live
-            for m in range(members):
-                old = state[s % 2, m, pl.ds(pad + TILE * t + old_by, TILE), :]
-                new = recv[s][pl.ds(window + m * slab, TILE), :]
-                value = jnp.where(fresh, new, old)
-                if last:
-                    value = jnp.where(filled, value, 0.0)
-                    out_ref[first + m, TILE * t : TILE * t + TILE, :] = value
-                else:
-                    at = pad + TILE * t
-                    state[1 - s % 2, m, at : at + TILE, :] = value
+            old = state[s % 2, pl.ds(pad + TILE * t + old_by, TILE), :]
+            value = jnp.where(fresh, arrived[pl.ds(window, TILE), :], old)
+            if s == sections - 1:
+                value = jnp.where(row + TILE * t < live, value, 0.0)
+                out_ref[m, TILE * t : TILE * t + TILE, :] = value
+            else:
+                at = pad + TILE * t
+                state[1 - s % 2, at : at + TILE, :] = value
 
     def merge_leaf(s, leaf):
         _, old_by, new_at, got = plans[s]
         old = pltpu.roll(leaf, lax.rem(slots - old_by, slots), 1)
-        new = pltpu.roll(recv_a[s][0:TILE, :], lax.rem(new_at, slots), 1)
+        new = pltpu.roll(arrivals[s * MEMBERS + LEAF_CHAIN][0:TILE, :], lax.rem(new_at, slots), 1)
         index = lane - new_at
         return jnp.where((index >= 0) & (index < got), new, old)
 
-    loads[0].wait()
-    loads[1].wait()
-    loads[2].wait()
+    leaf = jnp.broadcast_to(leaf_ref[...], (TILE, slots)).astype(jnp.float32)
     pl.semaphore_wait(barrier, sections)
-
-    first = emit(0, 0, leaf)
-    second = emit(0, 1, leaf)
-    started = []
-    for s in range(sections):
-        first.wait_recv()
-        started += [first, second]
-        leaf = merge_leaf(s, leaf)
-        merge(s, 0)
+    copies = {}
+    for n, m in enumerate(CHAIN_ORDER):
+        loads[n].wait()
+        copies[0, m] = emit(0, m, leaf)
+    events = [(SKEW * s + n, s, m) for s in range(sections) for n, m in enumerate(CHAIN_ORDER)]
+    for _, s, m in sorted(events):
+        copies[s, m].wait_recv()
+        if m == LEAF_CHAIN:
+            leaf = merge_leaf(s, leaf)
+        merge(s, m)
         if s + 1 < sections:
-            first = emit(s + 1, 0, leaf)
-        second.wait_recv()
-        merge(s, 1)
-        if s + 1 < sections:
-            second = emit(s + 1, 1, leaf)
+            copies[s + 1, m] = emit(s + 1, m, leaf)
     leaf_out_ref[...] = jnp.where(lane < live, leaf, -1.0)
-    for copy in started:
+    for copy in copies.values():
         copy.wait_send()
 
 
@@ -297,26 +281,22 @@
     any_space = pl.BlockSpec(memory_space=pl.ANY)
     vmem = pl.BlockSpec(memory_space=pltpu.VMEM)
     smem = pl.BlockSpec(memory_space=pltpu.SMEM)
-    rows_a = TILE + 4 * slab
-    rows_b = TILE + 3 * slab
     moved, leaf = pl.pallas_call(
         functools.partial(exchange_kernel, sizes),
         out_shape=(
-            jax.ShapeDtypeStruct((7, slots, part), f32),
+            jax.ShapeDtypeStruct((MEMBERS, slots, part), f32),
             jax.ShapeDtypeStruct((TILE, slots), f32),
         ),
         in_specs=[smem, smem, vmem, any_space, any_space, any_space],
         out_specs=(vmem, vmem),
         scratch_shapes=[
-            pltpu.VMEM((2, 4, slots + 2 * slab, part), f32),
-            pltpu.VMEM((2, 3, slots + 2 * slab, part), f32),
-            pltpu.VMEM((sections, rows_a, part), f32),
-            pltpu.VMEM((sections, rows_b, part), f32),
-            pltpu.SemaphoreType.DMA((3,)),
-            pltpu.SemaphoreType.DMA((sections, 2)),
-            pltpu.SemaphoreType.DMA((sections, 2)),
+            pltpu.VMEM((sections, MEMBERS, TILE + slab, part), f32),
+            pltpu.SemaphoreType.DMA((MEMBERS,)),
+            pltpu.SemaphoreType.DMA((sections, MEMBERS)),
+            pltpu.SemaphoreType.DMA((sections, MEMBERS)),
         ]
-        + [pltpu.VMEM((r + TILE, part), f32) for _ in range(sections) for r in (rows_a, rows_b)],
+        + [pltpu.VMEM((2, slots + 2 * slab, part), f32)] * MEMBERS
+        + [pltpu.VMEM((slab + 2 * TILE, part), f32)] * (sections * MEMBERS),
         compiler_params=pltpu.CompilerParams(collective_id=0, has_side_effects=True),
     )(live_counts, send_counts, leaf_ids.reshape(1, slots), positions, charges, velocities)
 

time: 31 us -> 31.6 us (1.019)
  Pallas kernels: 30.2 us -> 30.8 us
    pallas_call x1, Pallas kernels: 26.2 us -> 26.8 us  [per_device(): pl.pallas_call(functools.partial(exchange_kernel, sizes), out_shape=(jax....]
where the time goes in v1:
time: 31.6 us; the launch traced here: 31.4 us
  Pallas kernels  30.8 us (97%)
  between operations  0.64 us (2%)
    pallas_call x1, Pallas kernels, per_device(): pl.pallas_call(functools.partial(exchange_kernel, sizes), out_shape=(jax....  26.8 us
    pallas_call x1, Pallas kernels, per_device(): pl.pallas_call(functools.partial(moments_kernel, ORDER, LEVEL), out_shape...  4.01 us

profile of v1, /device:TPU:0, one launch (start us, length us, event | category | flops | bytes accessed | tf_op | source)
XLA Modules:
  0.0 31.4 jit_solution(14969738390414667350)
XLA Ops:
  0.6 26.8 %shard_map.127 = (f32[7,128,128]{2,1,0:T(8,128)}, f32[8,128]{1,0:T(8,128)}) custom-call(s32[32]{0:T(128)} %live_ref.1, s32[5,32]{1,0:T(8,128)} %sends_ref.1, s32[1,128]{1,0:T(1,128)} %bitcast.2, f32[3,128,128]{2,1,0:T(8,128)} %pos_ref.1, f32[128,128]{1,0:T(8,128)} %chg_ref.1, f32[3,128,128]{2,1,0:T(8,128)} %vel_ref.1), custom_call_target="tpu_custom_call" | custom-call | tf_op jit(solution)/shard_map/pallas_call | solution.py:284
  27.4 4.0 %shard_map.128 = (f32[3,128,128]{2,1,0:T(8,128)}, f32[128,128]{1,0:T(8,128)}, f32[3,128,128]{2,1,0:T(8,128)}, s32[1,128]{1,0:T(1,128)}, f32[286,128]{1,0:T(8,128)}, /*index=5*/f32[286,128]{1,0:T(8,128)}) custom-call(f32[7,128,128]{2,1,0:T(8,128)} %get-tuple-element.14.moved_ref, f32[8,128]{1,0:T(8,128)} %get-tuple-element.15.leaf_ref, ...), custom_call_target="tpu_custom_call" | custom-call | tf_op jit(solution)/shard_map/pallas_call | solution.py:306

commit v2 on v1

--- a/solution.py
+++ b/solution.py
@@ -16,7 +16,6 @@
 MEMBERS = 7
 LEAF_CHAIN = 3
 CHAIN_ORDER = (3, 0, 1, 2, 4, 5, 6)
-SKEW = 3
 
 
 def exponents(max_order):
@@ -52,7 +51,9 @@
     out_ref,
     leaf_out_ref,
     slabs,
+    result,
     in_sem,
+    out_sem,
     send_sem,
     recv_sem,
     *buffers,
@@ -113,13 +114,31 @@
     lane = lax.broadcasted_iota(jnp.int32, (TILE, slots), 1)
     row = lax.broadcasted_iota(jnp.int32, (TILE, part), 0)
 
+    def joined(s, m, first):
+        state, arrived = states[m], arrivals[s * MEMBERS + m]
+        _, old_by, new_at, got = plans[s]
+        base = first - new_at
+        index = row + base
+        fresh = (index >= 0) & (index < got)
+        window = jnp.clip(base, -TILE, slab) + TILE
+        place = jnp.minimum(pad + first + old_by, 2 * pad + slots - TILE)
+        return jnp.where(
+            fresh, arrived[pl.ds(window, TILE), :], state[s % 2, pl.ds(place, TILE), :]
+        )
+
     def emit(s, m, leaf):
         start = plans[s][0]
         first = TILE
         if m == LEAF_CHAIN:
             slabs[s, m, 0:TILE, :] = pltpu.roll(leaf, lax.rem(slots - start, slots), 1)
             first = 0
-        slabs[s, m, TILE : TILE + slab, :] = states[m][s % 2, pl.ds(pad + start, slab), :]
+        for t in range(slab // TILE):
+            at = TILE * t
+            if s == 0:
+                value = states[m][0, pl.ds(pad + start + at, TILE), :]
+            else:
+                value = joined(s - 1, m, start + at)
+            slabs[s, m, TILE + at : 2 * TILE + at, :] = value
         copy = pltpu.make_async_remote_copy(
             src_ref=slabs.at[s, m, first : TILE + slab, :],
             dst_ref=arrivals[s * MEMBERS + m].at[first : TILE + slab, :],
@@ -132,25 +151,20 @@
         return copy
 
     def merge(s, m):
-        state, arrived = states[m], arrivals[s * MEMBERS + m]
-        _, old_by, new_at, got = plans[s]
         for t in range(slots // TILE):
-            base = TILE * t - new_at
-            window = jnp.clip(base, -TILE, slab) + TILE
-            index = row + base
-            fresh = (index >= 0) & (index < got)
-            old = state[s % 2, pl.ds(pad + TILE * t + old_by, TILE), :]
-            value = jnp.where(fresh, arrived[pl.ds(window, TILE), :], old)
+            at = TILE * t
+            value = joined(s, m, at)
             if s == sections - 1:
-                value = jnp.where(row + TILE * t < live, value, 0.0)
-                out_ref[m, TILE * t : TILE * t + TILE, :] = value
+                value = jnp.where(row + at < live, value, 0.0)
+                result[m, at : at + TILE, :] = value
             else:
-                at = pad + TILE * t
-                state[1 - s % 2, at : at + TILE, :] = value
-
-    def merge_leaf(s, leaf):
-        _, old_by, new_at, got = plans[s]
-        old = pltpu.roll(leaf, lax.rem(slots - old_by, slots), 1)
+                states[m][1 - s % 2, pad + at : pad + at + TILE, :] = value
+
+    def shifted_leaf(s, leaf):
+        return pltpu.roll(leaf, lax.rem(slots - plans[s][1], slots), 1)
+
+    def merge_leaf(s, old):
+        _, _, new_at, got = plans[s]
         new = pltpu.roll(arrivals[s * MEMBERS + LEAF_CHAIN][0:TILE, :], lax.rem(new_at, slots), 1)
         index = lane - new_at
         return jnp.where((index >= 0) & (index < got), new, old)
@@ -161,17 +175,27 @@
     for n, m in enumerate(CHAIN_ORDER):
         loads[n].wait()
         copies[0, m] = emit(0, m, leaf)
-    events = [(SKEW * s + n, s, m) for s in range(sections) for n, m in enumerate(CHAIN_ORDER)]
-    for _, s, m in sorted(events):
-        copies[s, m].wait_recv()
-        if m == LEAF_CHAIN:
-            leaf = merge_leaf(s, leaf)
-        merge(s, m)
+    stores = []
+    for s in range(sections):
+        old_leaf = shifted_leaf(s, leaf)
+        for m in CHAIN_ORDER:
+            copies[s, m].wait_recv()
+            if m == LEAF_CHAIN:
+                leaf = merge_leaf(s, old_leaf)
+            if s + 1 < sections:
+                copies[s + 1, m] = emit(s + 1, m, leaf)
+            else:
+                merge(s, m)
+                stores.append(pltpu.make_async_copy(result.at[m], out_ref.at[m], out_sem.at[m]))
+                stores[-1].start()
         if s + 1 < sections:
-            copies[s + 1, m] = emit(s + 1, m, leaf)
+            for m in CHAIN_ORDER:
+                merge(s, m)
     leaf_out_ref[...] = jnp.where(lane < live, leaf, -1.0)
     for copy in copies.values():
         copy.wait_send()
+    for store in stores:
+        store.wait()
 
 
 def moments_kernel(
@@ -288,9 +312,11 @@
             jax.ShapeDtypeStruct((TILE, slots), f32),
         ),
         in_specs=[smem, smem, vmem, any_space, any_space, any_space],
-        out_specs=(vmem, vmem),
+        out_specs=(any_space, vmem),
         scratch_shapes=[
             pltpu.VMEM((sections, MEMBERS, TILE + slab, part), f32),
+            pltpu.VMEM((MEMBERS, slots, part), f32),
+            pltpu.SemaphoreType.DMA((MEMBERS,)),
             pltpu.SemaphoreType.DMA((MEMBERS,)),
             pltpu.SemaphoreType.DMA((sections, MEMBERS)),
             pltpu.SemaphoreType.DMA((sections, MEMBERS)),

time: 31.6 us -> 28.2 us (0.89)
  Pallas kernels: 30.8 us -> 27.3 us
    pallas_call x1, Pallas kernels: 26.8 us -> 23.3 us  [per_device(): pl.pallas_call(functools.partial(exchange_kernel, sizes), out_shape=(jax....]
where the time goes in v2:
time: 28.2 us; the launch traced here: 28 us
  Pallas kernels  27.3 us (97%)
  between operations  0.64 us (2%)
    pallas_call x1, Pallas kernels, per_device(): pl.pallas_call(functools.partial(exchange_kernel, sizes), out_shape=(jax....  23.3 us
    pallas_call x1, Pallas kernels, per_device(): pl.pallas_call(functools.partial(moments_kernel, ORDER, LEVEL), out_shape...  4.01 us

profile of v2, /device:TPU:0, one launch (start us, length us, event | category | flops | bytes accessed | tf_op | source)
XLA Modules:
  0.0 28.0 jit_solution(1971330211182342264)
XLA Ops:
  0.6 23.3 %shard_map.127 = (f32[7,128,128]{2,1,0:T(8,128)}, f32[8,128]{1,0:T(8,128)}) custom-call(s32[32]{0:T(128)} %live_ref.1, s32[5,32]{1,0:T(8,128)} %sends_ref.1, s32[1,128]{1,0:T(1,128)} %bitcast.2, f32[3,128,128]{2,1,0:T(8,128)} %pos_ref.1, f32[128,128]{1,0:T(8,128)} %chg_ref.1, f32[3,128,128]{2,1,0:T(8,128)} %vel_ref.1), custom_call_target="tpu_custom_call" | custom-call | tf_op jit(solution)/shard_map/pallas_call | solution.py:308
  24.0 4.0 %shard_map.128 = (f32[3,128,128]{2,1,0:T(8,128)}, f32[128,128]{1,0:T(8,128)}, f32[3,128,128]{2,1,0:T(8,128)}, s32[1,128]{1,0:T(1,128)}, f32[286,128]{1,0:T(8,128)}, /*index=5*/f32[286,128]{1,0:T(8,128)}) custom-call(f32[7,128,128]{2,1,0:T(8,128)} %get-tuple-element.14.moved_ref, f32[8,128]{1,0:T(8,128)} %get-tuple-element.15.leaf_ref, ...), custom_call_target="tpu_custom_call" | custom-call | tf_op jit(solution)/shard_map/pallas_call | solution.py:332
